TPU v7x, 32 devices: a whole 2x2x4 slice. The times are simulated.
32 devices in a mesh: rve: 4 (over y, x), slab: 8 (over z, core).
Axes of the slice: x: 2, y: 2, z: 4, core: 2. Of those that a mesh axis runs over, the one named last changes fastest.
Arguments:
- displacement: float32 [32, 3, 128, 256], P('slab', None, 'rve'), parts along dimension 2, may hold values from -6 to 6
- load: float32 [32, 3, 128, 256], P('slab', None, 'rve'), parts along dimension 2, may hold values from -24 to 24
- phase: int32 [32, 128, 256], P('slab', 'rve'), parts along dimension 1, may hold values from 0 to 2
- moduli: float32 [2, 3], replicated, may hold values from 0.5 to 4
Outputs:
- solution: float32 [32, 3, 128, 256], P('slab', None, 'rve'), parts along dimension 2
- residual: float32 [32, 3, 128, 256], P('slab', None, 'rve'), parts along dimension 2
There are 4 independent parts, one for each index of `rve`. A program takes and returns all parts, laid end to end along the dimension named above; an argument that names none is the same for every part. Nothing has to cross between parts.
All inputs are finite; a program needn't handle non-finite values.
Results may differ from a plain program's by a relative error of at most 0.00002.
Values sent between devices are 32-bit elements; how exact they have to be, the bound alone decides.
A program may use at most 64 MiB of HBM per device.

v0:
```python
import functools

import jax
import jax.numpy as jnp
from jax import lax
from jax.experimental import pallas as pl
from jax.experimental.pallas import tpu as pltpu
from jax.sharding import PartitionSpec as P

SWEEPS = 6
MESH = pl.DeviceIdType.MESH
ROWS = 8

STRESS = ((0, 3, 4), (3, 1, 5), (4, 5, 2))


def shift_next(value, axis):
    return pltpu.roll(value, value.shape[axis] - 1, axis)


def shift_prev(value, axis):
    return pltpu.roll(value, 1, axis)


def kernel(
    peers, disp, load, phase, moduli, out, rest,
    u, ld, ph, lam, mu, mu2, inv, fwd, st,
    in_sem, edge_send, edge_recv, send_sem, recv_sem,
):
    local, _, nx, ny = disp.shape
    phases = moduli.shape[1]
    me = lax.axis_index("slab")
    above = lax.rem(me + 1, peers)
    below = lax.rem(me + peers - 1, peers)

    first = pltpu.make_async_copy(disp, u.at[0, pl.ds(2, local)], in_sem.at[0])
    second = pltpu.make_async_copy(phase, ph.at[pl.ds(2, local)], in_sem.at[1])
    third = pltpu.make_async_copy(load, ld.at[pl.ds(1, local)], in_sem.at[2])
    first.start()
    second.start()
    third.start()

    barrier = pltpu.get_barrier_semaphore()
    for peer in (below, above):
        pl.semaphore_signal(barrier, inc=1, device_id={"slab": peer}, device_id_type=MESH)
    pl.semaphore_wait(barrier, 2)

    edges = []

    def edge(src, dst, peer):
        at = len(edges)
        copy = pltpu.make_async_remote_copy(
            src_ref=src, dst_ref=dst, send_sem=edge_send.at[at], recv_sem=edge_recv.at[at],
            device_id={"slab": peer}, device_id_type=MESH,
        )
        edges.append(copy)
        return copy

    near_u = [edge(u.at[0, local + 1], u.at[0, 1], above), edge(u.at[0, 2], u.at[0, local + 2], below)]
    near_ph = [edge(ph.at[local + 1], ph.at[1], above), edge(ph.at[2], ph.at[local + 2], below)]
    far_u = [edge(u.at[0, local], u.at[0, 0], above), edge(u.at[0, 3], u.at[0, local + 3], below)]
    far_ph = [edge(ph.at[local], ph.at[0], above)]
    far_ld = [edge(ld.at[local], ld.at[0], above), edge(ld.at[1], ld.at[local + 1], below)]
    closing = (me == peers - 1, me == 0)

    def far(way):
        far_u[way].start()
        if way == 0:
            far_ph[0].start()
        far_ld[way].start()

    first.wait()
    for copy in near_u:
        copy.start()
    second.wait()
    for copy in near_ph:
        copy.start()
    third.wait()
    for way in range(2):

        @pl.when(closing[way])
        def _():
            far(way)

    def sent(sweep, way):
        src, dst, peer = ((local, 0, above), (3, local + 3, below))[way]
        return pltpu.make_async_remote_copy(
            src_ref=u.at[sweep, src], dst_ref=u.at[sweep, dst],
            send_sem=send_sem.at[sweep, way], recv_sem=recv_sem.at[sweep, way],
            device_id={"slab": peer}, device_id_type=MESH,
        )

    def material(k):
        for r in range(0, nx, ROWS):
            at = pl.ds(r, ROWS)
            kind = ph[k + 2, at, :]
            lame = jnp.zeros(kind.shape, jnp.float32)
            shear = jnp.zeros(kind.shape, jnp.float32)
            for index in range(phases):
                lame = jnp.where(kind == index, moduli[0, index] * 0.0625, lame)
                shear = jnp.where(kind == index, moduli[1, index] * 0.0625, shear)
            lam[k + 2, at, :] = lame
            mu[k + 2, at, :] = shear
            mu2[k + 2, at, :] = shear + shear

    def diagonal(n):
        total = (lam[n + 1] + 2.0 * mu2[n + 1]) + (lam[n + 2] + 2.0 * mu2[n + 2])
        total = total + shift_prev(total, 1)
        total = total + shift_prev(total, 0)
        inv[n + 1] = 0.5 / total

    def forward(sweep, n):
        for c in range(3):
            value = u[sweep, n + 2, c]
            moved = shift_next(value, 1)
            total, jump = value + moved, moved - value
            moved = shift_next(total, 0)
            fwd[n + 2, c] = moved - total
            fwd[n + 2, 6 + c] = moved + total
            fwd[n + 2, 3 + c] = jump + shift_next(jump, 0)

    def element(k):
        lo, hi = k + 2, k + 3
        for r in range(0, nx, ROWS):
            at = pl.ds(r, ROWS)
            gx = [fwd[lo, c, at, :] + fwd[hi, c, at, :] for c in range(3)]
            gy = [fwd[lo, 3 + c, at, :] + fwd[hi, 3 + c, at, :] for c in range(3)]
            gz = [fwd[hi, 6 + c, at, :] - fwd[lo, 6 + c, at, :] for c in range(3)]
            bulk = lam[lo, at, :] * (gx[0] + gy[1] + gz[2])
            two, one = mu2[lo, at, :], mu[lo, at, :]
            st[lo, 0, at, :] = bulk + two * gx[0]
            st[lo, 1, at, :] = bulk + two * gy[1]
            st[lo, 2, at, :] = bulk + two * gz[2]
            st[lo, 3, at, :] = one * (gy[0] + gx[1])
            st[lo, 4, at, :] = one * (gz[0] + gx[2])
            st[lo, 5, at, :] = one * (gz[1] + gy[2])

    def remain(n, c):
        lo, hi = n + 1, n + 2
        x, y, z = STRESS[c]
        px = st[lo, x] + st[hi, x]
        rz = st[lo, z] - st[hi, z]
        qy = st[lo, y] + st[hi, y]
        e = (rz - px) + shift_prev(rz + px, 0)
        b = qy + shift_prev(qy, 0)
        return ld[n + 1, c] - ((e - b) + shift_prev(e + b, 1))

    def advance(sweep, n):
        for c in range(3):
            u[sweep, n + 2, c] = u[sweep - 1, n + 2, c] + inv[n + 1] * remain(n, c)

    def finish(n):
        for c in range(3):
            rest[n, c] = remain(n, c)

    rims = (0, local - 1)
    seconds = (1, local - 2)

    def middle(sweep):
        for n in range(1, local - 1):
            forward(sweep, n)
        for k in range(1, local - 2):
            element(k)

    def join(sweep, side):
        forward(sweep, rims[side])
        element((0, local - 2)[side])

    def halo(sweep, side):
        forward(sweep - 1, (-2, local + 1)[side])
        element((-2, local)[side])
        advance(sweep, (-1, local)[side])

    def rim(sweep, side):
        forward(sweep, (-1, local)[side])
        element((-1, local - 1)[side])

    for k in range(local):
        material(k)
    for n in range(1, local):
        diagonal(n)
    middle(0)
    for side in range(2):
        join(0, side)
    for n in range(1, local - 1):
        advance(1, n)
    for way in range(2):

        @pl.when(closing[way])
        def _():
            sent(1, way).start()

    middle(1)
    for n in range(2, local - 2):
        advance(2, n)
    for side in range(2):
        near_u[side].wait_recv()
        near_ph[side].wait_recv()
        material((-1, local)[side])
        diagonal((0, local)[side])
        if side == 0:
            for way in range(2):

                @pl.when(jnp.logical_not(closing[way]))
                def _():
                    far(way)
                    sent(1, way).start()

        rim(0, side)
        advance(1, rims[side])
        join(1, side)
        advance(2, seconds[side])
        sent(2, 1 - side).start()

    def step(sweep, _):
        middle(sweep)
        for n in range(2, local - 2):
            advance(sweep + 1, n)
        for side in range(2):

            @pl.when(sweep == 2)
            def _():
                far_u[side].wait_recv()
                far_ld[side].wait_recv()
                if side == 0:
                    far_ph[0].wait_recv()
                    material(-2)
                    diagonal(-1)

            @pl.when(sweep > 2)
            def _():
                sent(sweep - 2, side).wait_recv()

            halo(sweep - 1, side)
            rim(sweep - 1, side)
            advance(sweep, rims[side])
            join(sweep, side)
            advance(sweep + 1, seconds[side])

            @pl.when(sweep + 1 < SWEEPS)
            def _():
                sent(sweep + 1, 1 - side).start()

        return 0

    lax.fori_loop(2, SWEEPS, step, 0)

    middle(SWEEPS)
    for n in range(2, local - 2):
        finish(n)
    for n in range(1, local - 1):
        out[n] = u[SWEEPS, n + 2]
    for side in range(2):
        sent(SWEEPS - 2, side).wait_recv()
        halo(SWEEPS - 1, side)
        rim(SWEEPS - 1, side)
        advance(SWEEPS, rims[side])
        join(SWEEPS, side)
        finish(seconds[side])
    for n in rims:
        out[n] = u[SWEEPS, n + 2]
    for side in range(2):
        sent(SWEEPS - 1, side).wait_recv()
        halo(SWEEPS, side)
        rim(SWEEPS, side)
        finish(rims[side])
    for copy in edges:
        copy.wait_send()
    for sweep in range(1, SWEEPS):
        for way in range(2):
            sent(sweep, way).wait_send()


def write_out(field, remain, out, rest, sem):
    copies = [pltpu.make_async_copy(field, out, sem.at[0]), pltpu.make_async_copy(remain, rest, sem.at[1])]
    for copy in copies:
        copy.start()
    for copy in copies:
        copy.wait()


def on_device(peers, displacement, load, phase, moduli):
    local, comps, nx, ny = displacement.shape
    plane = (nx, ny)
    hbm = pl.BlockSpec(memory_space=pl.ANY)
    f32 = jnp.float32
    vmem = pl.BlockSpec(memory_space=pltpu.VMEM)
    held = pl.pallas_call(
        functools.partial(kernel, peers),
        out_shape=[pltpu.VMEM(displacement.shape, f32)] * 2,
        in_specs=[hbm, hbm, hbm, pl.BlockSpec(memory_space=pltpu.SMEM)],
        out_specs=[vmem, vmem],
        scratch_shapes=[
            pltpu.VMEM((SWEEPS + 1, local + 4, comps) + plane, f32),
            pltpu.VMEM((local + 2, comps) + plane, f32),
            pltpu.VMEM((local + 3,) + plane, jnp.int32),
            pltpu.VMEM((local + 3,) + plane, f32),
            pltpu.VMEM((local + 3,) + plane, f32),
            pltpu.VMEM((local + 3,) + plane, f32),
            pltpu.VMEM((local + 2,) + plane, f32),
            pltpu.VMEM((local + 4, 9) + plane, f32),
            pltpu.VMEM((local + 3, 6) + plane, f32),
            pltpu.SemaphoreType.DMA((3,)),
            pltpu.SemaphoreType.DMA((9,)),
            pltpu.SemaphoreType.DMA((9,)),
            pltpu.SemaphoreType.DMA((SWEEPS + 1, 2)),
            pltpu.SemaphoreType.DMA((SWEEPS + 1, 2)),
        ],
        compiler_params=pltpu.CompilerParams(collective_id=0, has_side_effects=True),
    )(displacement, load, phase, moduli)
    return pl.pallas_call(
        write_out,
        out_shape=[jax.ShapeDtypeStruct(displacement.shape, f32)] * 2,
        in_specs=[hbm, hbm],
        out_specs=[hbm, hbm],
        scratch_shapes=[pltpu.SemaphoreType.DMA((2,))],
    )(*[pltpu.with_memory_space_constraint(one, pltpu.VMEM) for one in held])


def solution(mesh):
    in_specs = (
        P("slab", None, "rve", None),
        P("slab", None, "rve", None),
        P("slab", "rve", None),
        P(),
    )
    out_specs = (P("slab", None, "rve", None), P("slab", None, "rve", None))
    return jax.shard_map(
        functools.partial(on_device, mesh.shape["slab"]),
        mesh=mesh, in_specs=in_specs, out_specs=out_specs, check_vma=False,
    )
```

profile of v0, /device:TPU:0, one launch (start us, length us, event | category | flops | bytes accessed | tf_op | source)
XLA Modules:
  0.0 27.5 jit_solution(8999263185373000826)
XLA Ops:
  0.6 26.0 %shard_map.59 = (f32[4,3,32,256]{3,2,1,0:T(8,128)S(1)}, f32[4,3,32,256]{3,2,1,0:T(8,128)S(1)}) custom-call(f32[4,3,32,256]{3,2,1,0:T(8,128)} %disp.1, f32[4,3,32,256]{3,2,1,0:T(8,128)} %load.1, s32[4,32,256]{2,1,0:T(8,128)} %phase.1, f32[2,3]{1,0:T(2,128)} %moduli.1), custom_call_target="tpu_custom_call" | custom-call | tf_op jit(solution)/shard_map/pallas_call | solution.py:288
  26.6 0.9 %shard_map.60 = (f32[4,3,32,256]{3,2,1,0:T(8,128)}, f32[4,3,32,256]{3,2,1,0:T(8,128)}) custom-call(f32[4,3,32,256]{3,2,1,0:T(8,128)S(1)} %get-tuple-element.4.field, f32[4,3,32,256]{3,2,1,0:T(8,128)S(1)} %get-tuple-element.5.remain), custom_call_target="tpu_custom_call" | custom-call | tf_op jit(solution)/shard_map/pallas_call | solution.py:311
where the time goes:
time: 27.7 us; the launch traced here: 27.5 us
  Pallas kernels  26.9 us (97%)
  between operations  0.64 us (2%)
    pallas_call x1, Pallas kernels, on_device(): pl.pallas_call(functools.partial(kernel, peers), out_shape=[pltpu.VMEM(di...  26 us
    pallas_call x1, Pallas kernels, on_device(): pl.pallas_call(write_out, out_shape=[jax.ShapeDtypeStruct(displacement.sh...  0.89 us

commit v1 on v0

v1 whole, which is shorter than its diff:
```python
import functools

import jax
import jax.numpy as jnp
from jax import lax
from jax.experimental import pallas as pl
from jax.experimental.pallas import tpu as pltpu
from jax.sharding import PartitionSpec as P

SWEEPS = 6
MESH = pl.DeviceIdType.MESH
ROWS = 8

STRESS = ((0, 3, 4), (3, 1, 5), (4, 5, 2))


def shift_next(value, axis):
    return pltpu.roll(value, value.shape[axis] - 1, axis)


def shift_prev(value, axis):
    return pltpu.roll(value, 1, axis)


def kernel(
    peers, disp, load, phase, moduli, out, rest,
    raw, u, ld, ph, lam, mu, mu2, inv, fwd, st, near, held, pull,
    in_sem, out_send, out_recv, in_send, in_recv,
):
    local, _, nx, ny = disp.shape
    phases = moduli.shape[1]
    me = lax.axis_index("slab")
    odd = lax.rem(me, 2)
    sign = (1 - 2 * odd).astype(jnp.float32)
    outer = lax.rem(me + 2 * odd - 1 + peers, peers)
    inner = me + 1 - 2 * odd

    def plane(p):
        return jnp.where(odd == 1, local - 1 - p, p)

    loads = []

    def bring(src, dst):
        copy = pltpu.make_async_copy(src, dst, in_sem.at[len(loads)])
        loads.append(copy)
        copy.start()
        return copy

    order = [0, local - 1] + list(range(1, local - 1))
    nodes = {p: bring(disp.at[plane(p)], raw.at[p + 1]) for p in order[:2]}
    kinds = [bring(phase.at[k], ph.at[jnp.where(odd == 1, local - k, k + 2)]) for k in range(local)]
    nodes.update({p: bring(disp.at[plane(p)], raw.at[p + 1]) for p in order[2:]})
    bases = [bring(load.at[plane(p)], ld.at[p]) for p in range(local)]

    barrier = pltpu.get_barrier_semaphore()
    for peer in (outer, inner):
        pl.semaphore_signal(barrier, inc=1, device_id={"slab": peer}, device_id_type=MESH)
    pl.semaphore_wait(barrier, 2)

    def remote(src, dst, sends, recvs, at, peer):
        return pltpu.make_async_remote_copy(
            src_ref=src, dst_ref=dst, send_sem=sends.at[at], recv_sem=recvs.at[at],
            device_id={"slab": peer}, device_id_type=MESH,
        )

    out_copy = functools.partial(remote, sends=out_send, recvs=out_recv, peer=outer)
    in_copy = functools.partial(remote, sends=in_send, recvs=in_recv, peer=inner)
    out_node = out_copy(raw.at[1], raw.at[0], at=SWEEPS)
    out_far = out_copy(ph.at[2], ph.at[0], at=SWEEPS + 1)
    out_near = out_copy(ph.at[1], ph.at[1], at=SWEEPS + 2)
    in_kind = in_copy(ph.at[local + 1], ph.at[local + 1], at=SWEEPS + 1)
    pulls = [out_copy(held.at[s], pull.at[s], at=s) for s in range(SWEEPS)]

    def at_level(s, p):
        return raw.at[p + 1] if s == 0 else u.at[s - 1, p + 1]

    inners = [in_copy(at_level(s, local - 1), at_level(s, local), at=s) for s in range(SWEEPS + 1)]

    nodes[0].wait()
    out_node.start()
    nodes[local - 1].wait()
    inners[0].start()
    for copy in kinds:
        copy.wait()

    @pl.when(odd == 1)
    def _():
        out_near.start()

    @pl.when(odd == 0)
    def _():
        in_kind.start()

    def value_at(s, p, c):
        value = at_level(s, p)[c]
        if c == 2 and s == 0:
            return value * sign
        if c == 2 and p == local:
            return -value
        return value

    def material(e):
        for r in range(0, nx, ROWS):
            at = pl.ds(r, ROWS)
            kind = ph[e + 2, at, :]
            lame = jnp.zeros(kind.shape, jnp.float32)
            shear = jnp.zeros(kind.shape, jnp.float32)
            for index in range(phases):
                lame = jnp.where(kind == index, moduli[0, index] * 0.0625, lame)
                shear = jnp.where(kind == index, moduli[1, index] * 0.0625, shear)
            lam[e + 2, at, :] = lame
            mu[e + 2, at, :] = shear
            mu2[e + 2, at, :] = shear + shear

    def diagonal(p):
        total = (lam[p + 1] + 2.0 * mu2[p + 1]) + (lam[p + 2] + 2.0 * mu2[p + 2])
        total = total + shift_prev(total, 1)
        total = total + shift_prev(total, 0)
        inv[p + 1] = 0.5 / total

    def forward(s, p):
        for c in range(3):
            value = value_at(s, p, c)
            moved = shift_next(value, 1)
            total, jump = value + moved, moved - value
            moved = shift_next(total, 0)
            fwd[p + 1, c] = moved - total
            fwd[p + 1, 6 + c] = moved + total
            fwd[p + 1, 3 + c] = jump + shift_next(jump, 0)

    def element(e, half=False, into=None):
        lo, hi = e + 1, e + 2
        to = e + 2 if into is None else into
        for r in range(0, nx, ROWS):
            at = pl.ds(r, ROWS)
            gx, gy, gz = ([fwd[hi, 3 * a + c, at, :] for c in range(3)] for a in range(3))
            if not half:
                gx = [gx[c] + fwd[lo, c, at, :] for c in range(3)]
                gy = [gy[c] + fwd[lo, 3 + c, at, :] for c in range(3)]
                gz = [gz[c] - fwd[lo, 6 + c, at, :] for c in range(3)]
            bulk = lam[e + 2, at, :] * (gx[0] + gy[1] + gz[2])
            two, one = mu2[e + 2, at, :], mu[e + 2, at, :]
            st[to, 0, at, :] = bulk + two * gx[0]
            st[to, 1, at, :] = bulk + two * gy[1]
            st[to, 2, at, :] = bulk + two * gz[2]
            st[to, 3, at, :] = one * (gy[0] + gx[1])
            st[to, 4, at, :] = one * (gz[0] + gx[2])
            st[to, 5, at, :] = one * (gz[1] + gy[2])

    def force(px, qy, rz):
        e = (rz - px) + shift_prev(rz + px, 0)
        b = qy + shift_prev(qy, 0)
        return (e - b) + shift_prev(e + b, 1)

    def internal(p, c):
        lo, hi = p + 1, p + 2
        x, y, z = STRESS[c]
        return force(st[lo, x] + st[hi, x], st[lo, y] + st[hi, y], st[lo, z] - st[hi, z])

    def based(p, c):
        return ld[p, c] * sign if c == 2 else ld[p, c]

    def settle(s, p, c, value):
        u[s - 1, p + 1, c] = value
        if s == SWEEPS and 0 <= p < local:
            out[plane(p), c] = value * sign if c == 2 else value

    def advance(s, p):
        for c in range(3):
            remain = based(p, c) - internal(p, c)
            if s > SWEEPS:
                rest[plane(p), c] = remain * sign if c == 2 else remain
            else:
                settle(s, p, c, value_at(s - 1, p, c) + inv[p + 1] * remain)

    def prepare(s):
        element(-2, half=True)
        for c in range(3):
            near[c] = value_at(s - 1, -1, c) - inv[0] * internal(-1, c)

    def land(s):
        for c in range(3):
            drawn = inv[0] * pull[s - 1, c]
            settle(s, -1, c, near[c] - drawn if c == 2 else near[c] + drawn)

    spare = local + 2

    def offer(s):
        element(0, half=True, into=spare)
        for c in range(3):
            x, y, z = STRESS[c]
            held[s, c] = based(0, c) - force(st[spare, x], st[spare, y], -st[spare, z])
        pulls[s].start()

    def outer_part(t):
        if t == -1:
            out_node.wait_recv()

            @pl.when(odd == 0)
            def _():
                out_near.wait_recv()

            material(-1)
            diagonal(0)
        if 0 <= t < SWEEPS:
            pulls[t].wait_recv()
            land(t + 1)
        if -1 <= t < SWEEPS:
            forward(t + 1, -1)
            element(-1)
            advance(t + 2, 0)

    def middle_part(t):
        if 0 <= t + 2 <= SWEEPS:
            forward(t + 2, 0)
            element(0)
            advance(t + 3, 1)

    def offer_part(t):
        if 0 <= t + 3 <= SWEEPS:
            forward(t + 3, 1)
        if 0 <= t + 3 < SWEEPS:
            offer(t + 3)

    def inner_part(t):
        for p in range(2, local):
            if 0 <= t + p + 1 <= SWEEPS:
                if p > 2:
                    forward(t + p + 1, p - 1)
                element(p - 1)
                if p == local - 1:
                    inners[t + p + 1].wait_recv()
                    if t + p + 1 == 0:

                        @pl.when(odd == 1)
                        def _():
                            in_kind.wait_recv()

                        material(local - 1)
                        diagonal(local - 1)
                    forward(t + p + 1, local)
                    element(local - 1)
                advance(t + p + 2, p)
                if p == local - 1 and t + p + 2 <= SWEEPS:
                    inners[t + p + 2].start()
        if 0 <= t + local + 1 <= SWEEPS:
            forward(t + local + 1, local - 1)

    def after_part(t):
        if t == -1:
            out_far.wait_recv()
            material(-2)
            diagonal(-1)
        if -1 <= t < SWEEPS - 1:
            prepare(t + 2)

    for p in range(local - 1):
        material(p)
    for p in range(1, local - 1):
        diagonal(p)
    for copy in [nodes[p] for p in order[2:]] + bases:
        copy.wait()
    for t in range(-local - 1, SWEEPS):
        outer_part(t)
        middle_part(t)
        offer_part(t)
        if t == -3:
            out_far.start()
        inner_part(t)
        after_part(t)

    out_node.wait_send()
    out_far.wait_send()

    @pl.when(odd == 1)
    def _():
        out_near.wait_send()

    @pl.when(odd == 0)
    def _():
        in_kind.wait_send()

    for copy in pulls + inners:
        copy.wait_send()


def write_out(field, remain, out, rest, sem):
    copies = [pltpu.make_async_copy(field, out, sem.at[0]), pltpu.make_async_copy(remain, rest, sem.at[1])]
    for copy in copies:
        copy.start()
    for copy in copies:
        copy.wait()


def on_device(peers, displacement, load, phase, moduli):
    local, comps, nx, ny = displacement.shape
    plane = (nx, ny)
    hbm = pl.BlockSpec(memory_space=pl.ANY)
    f32 = jnp.float32
    vmem = pl.BlockSpec(memory_space=pltpu.VMEM)
    held = pl.pallas_call(
        functools.partial(kernel, peers),
        out_shape=[pltpu.VMEM(displacement.shape, f32)] * 2,
        in_specs=[hbm, hbm, hbm, pl.BlockSpec(memory_space=pltpu.SMEM)],
        out_specs=[vmem, vmem],
        scratch_shapes=[
            pltpu.VMEM((local + 2, comps) + plane, f32),
            pltpu.VMEM((SWEEPS, local + 2, comps) + plane, f32),
            pltpu.VMEM((local, comps) + plane, f32),
            pltpu.VMEM((local + 2,) + plane, jnp.int32),
            pltpu.VMEM((local + 2,) + plane, f32),
            pltpu.VMEM((local + 2,) + plane, f32),
            pltpu.VMEM((local + 2,) + plane, f32),
            pltpu.VMEM((local + 1,) + plane, f32),
            pltpu.VMEM((local + 2, 9) + plane, f32),
            pltpu.VMEM((local + 3, 6) + plane, f32),
            pltpu.VMEM((comps,) + plane, f32),
            pltpu.VMEM((SWEEPS, comps) + plane, f32),
            pltpu.VMEM((SWEEPS, comps) + plane, f32),
            pltpu.SemaphoreType.DMA((3 * local,)),
            pltpu.SemaphoreType.DMA((SWEEPS + 3,)),
            pltpu.SemaphoreType.DMA((SWEEPS + 3,)),
            pltpu.SemaphoreType.DMA((SWEEPS + 2,)),
            pltpu.SemaphoreType.DMA((SWEEPS + 2,)),
        ],
        compiler_params=pltpu.CompilerParams(collective_id=0, has_side_effects=True),
    )(displacement, load, phase, moduli)
    return pl.pallas_call(
        write_out,
        out_shape=[jax.ShapeDtypeStruct(displacement.shape, f32)] * 2,
        in_specs=[hbm, hbm],
        out_specs=[hbm, hbm],
        scratch_shapes=[pltpu.SemaphoreType.DMA((2,))],
    )(*[pltpu.with_memory_space_constraint(one, pltpu.VMEM) for one in held])


def solution(mesh):
    in_specs = (
        P("slab", None, "rve", None),
        P("slab", None, "rve", None),
        P("slab", "rve", None),
        P(),
    )
    out_specs = (P("slab", None, "rve", None), P("slab", None, "rve", None))
    return jax.shard_map(
        functools.partial(on_device, mesh.shape["slab"]),
        mesh=mesh, in_specs=in_specs, out_specs=out_specs, check_vma=False,
    )
```

time: 27.7 us -> 25.1 us (0.906)
  Pallas kernels: 26.9 us -> 24.4 us
    pallas_call x1, Pallas kernels: 26 us -> 23.5 us  [on_device(): pl.pallas_call(functools.partial(kernel, peers), out_shape=[pltpu.VMEM(di...]
where the time goes in v1:
time: 25.1 us; the launch traced here: 25 us
  Pallas kernels  24.4 us (97%)
  between operations  0.64 us (3%)
    pallas_call x1, Pallas kernels, on_device(): pl.pallas_call(functools.partial(kernel, peers), out_shape=[pltpu.VMEM(di...  23.5 us
    pallas_call x1, Pallas kernels, on_device(): pl.pallas_call(write_out, out_shape=[jax.ShapeDtypeStruct(displacement.sh...  0.89 us

profile of v1, /device:TPU:0, one launch (start us, length us, event | category | flops | bytes accessed | tf_op | source)
XLA Modules:
  0.0 25.0 jit_solution(12861270765842691219)
XLA Ops:
  0.6 23.5 %shard_map.59 = (f32[4,3,32,256]{3,2,1,0:T(8,128)S(1)}, f32[4,3,32,256]{3,2,1,0:T(8,128)S(1)}) custom-call(f32[4,3,32,256]{3,2,1,0:T(8,128)} %disp.1, f32[4,3,32,256]{3,2,1,0:T(8,128)} %load.1, s32[4,32,256]{2,1,0:T(8,128)} %phase.1, f32[2,3]{1,0:T(2,128)} %moduli.1), custom_call_target="tpu_custom_call" | custom-call | tf_op jit(solution)/shard_map/pallas_call | solution.py:301
  24.1 0.9 %shard_map.60 = (f32[4,3,32,256]{3,2,1,0:T(8,128)}, f32[4,3,32,256]{3,2,1,0:T(8,128)}) custom-call(f32[4,3,32,256]{3,2,1,0:T(8,128)S(1)} %get-tuple-element.4.field, f32[4,3,32,256]{3,2,1,0:T(8,128)S(1)} %get-tuple-element.5.remain), custom_call_target="tpu_custom_call" | custom-call | tf_op jit(solution)/shard_map/pallas_call | solution.py:328

commit v2 on v1

--- a/solution.py
+++ b/solution.py
@@ -22,66 +22,98 @@
     return pltpu.roll(value, 1, axis)
 
 
+def slopes(value):
+    moved = shift_next(value, 1)
+    total, jump = value + moved, moved - value
+    moved = shift_next(total, 0)
+    return moved - total, jump + shift_next(jump, 0), moved + total
+
+
+def stresses(gx, gy, gz, lam, mu, mu2):
+    bulk = lam * (gx[0] + gy[1] + gz[2])
+    return (
+        bulk + mu2 * gx[0], bulk + mu2 * gy[1], bulk + mu2 * gz[2],
+        mu * (gy[0] + gx[1]), mu * (gz[0] + gx[2]), mu * (gz[1] + gy[2]),
+    )
+
+
+def force(px, qy, rz):
+    e = (rz - px) + shift_prev(rz + px, 0)
+    b = qy + shift_prev(qy, 0)
+    return (e - b) + shift_prev(e + b, 1)
+
+
+def plane_of(odd, local, p):
+    return jnp.where(odd == 1, local - 1 - p, p)
+
+
 def kernel(
-    peers, disp, load, phase, moduli, out, rest,
-    raw, u, ld, ph, lam, mu, mu2, inv, fwd, st, near, held, pull,
-    in_sem, out_send, out_recv, in_send, in_recv,
+    peers, disp, load, phase, table, out, rest, rim_u, rim_m,
+    moduli, raw, u, ld, ph, lam, mu, mu2, inv, fwd, st, near, held, pull,
+    in_sem, send_sem, recv_sem,
 ):
     local, _, nx, ny = disp.shape
-    phases = moduli.shape[1]
+    phases = table.shape[1]
     me = lax.axis_index("slab")
     odd = lax.rem(me, 2)
+    closing = jnp.logical_or(me == 0, me == peers - 1)
     sign = (1 - 2 * odd).astype(jnp.float32)
     outer = lax.rem(me + 2 * odd - 1 + peers, peers)
     inner = me + 1 - 2 * odd
 
     def plane(p):
-        return jnp.where(odd == 1, local - 1 - p, p)
-
-    loads = []
-
-    def bring(src, dst):
-        copy = pltpu.make_async_copy(src, dst, in_sem.at[len(loads)])
-        loads.append(copy)
-        copy.start()
-        return copy
-
-    order = [0, local - 1] + list(range(1, local - 1))
-    nodes = {p: bring(disp.at[plane(p)], raw.at[p + 1]) for p in order[:2]}
-    kinds = [bring(phase.at[k], ph.at[jnp.where(odd == 1, local - k, k + 2)]) for k in range(local)]
-    nodes.update({p: bring(disp.at[plane(p)], raw.at[p + 1]) for p in order[2:]})
-    bases = [bring(load.at[plane(p)], ld.at[p]) for p in range(local)]
+        return plane_of(odd, local, p)
+
+    def bring(src, dst, at):
+        return pltpu.make_async_copy(src, dst, in_sem.at[at])
+
+    def bring_node(p, at):
+        return bring(disp.at[plane(p)], raw.at[p + 1], at)
+
+    rim, hub, consts = bring_node(0, 0), bring_node(local - 1, 1), bring(table, moduli, 2)
+    kinds = bring(phase, ph.at[pl.ds(2, local)], 3)
+    middles = bring(disp.at[pl.ds(1, local - 2)], raw.at[pl.ds(2, local - 2)], 4)
+    bases = bring(load, ld, 5)
+    rim.start()
+    hub.start()
+    for k in range(local):
+        bring(phase.at[k], ph.at[jnp.where(odd == 1, local - k, k + 2)], 3).start()
+    consts.start()
+    for p in range(1, local - 1):
+        bring_node(p, 4).start()
+    for p in range(local):
+        bring(load.at[plane(p)], ld.at[p], 5).start()
 
     barrier = pltpu.get_barrier_semaphore()
     for peer in (outer, inner):
         pl.semaphore_signal(barrier, inc=1, device_id={"slab": peer}, device_id_type=MESH)
     pl.semaphore_wait(barrier, 2)
 
-    def remote(src, dst, sends, recvs, at, peer):
+    def remote(src, dst, send, recv, peer):
         return pltpu.make_async_remote_copy(
-            src_ref=src, dst_ref=dst, send_sem=sends.at[at], recv_sem=recvs.at[at],
+            src_ref=src, dst_ref=dst, send_sem=send_sem.at[send], recv_sem=recv_sem.at[recv],
             device_id={"slab": peer}, device_id_type=MESH,
         )
 
-    out_copy = functools.partial(remote, sends=out_send, recvs=out_recv, peer=outer)
-    in_copy = functools.partial(remote, sends=in_send, recvs=in_recv, peer=inner)
-    out_node = out_copy(raw.at[1], raw.at[0], at=SWEEPS)
-    out_far = out_copy(ph.at[2], ph.at[0], at=SWEEPS + 1)
-    out_near = out_copy(ph.at[1], ph.at[1], at=SWEEPS + 2)
-    in_kind = in_copy(ph.at[local + 1], ph.at[local + 1], at=SWEEPS + 1)
-    pulls = [out_copy(held.at[s], pull.at[s], at=s) for s in range(SWEEPS)]
+    out_node = remote(raw.at[1], raw.at[0], 2, SWEEPS, outer)
+    out_far = remote(ph.at[2], ph.at[0], 3, SWEEPS + 1, outer)
+    out_near = remote(ph.at[1], ph.at[1], 4, SWEEPS + 2, outer)
+    in_kind = remote(ph.at[local + 1], ph.at[local + 1], 4, SWEEPS + 2, inner)
+    pulls = [remote(held.at[s], pull.at[s], 0, s, outer) for s in range(SWEEPS)]
 
     def at_level(s, p):
         return raw.at[p + 1] if s == 0 else u.at[s - 1, p + 1]
 
-    inners = [in_copy(at_level(s, local - 1), at_level(s, local), at=s) for s in range(SWEEPS + 1)]
-
-    nodes[0].wait()
+    inners = [
+        remote(at_level(s, local - 1), at_level(s, local), 1 if s else 5, SWEEPS + 3 + s % 2, inner)
+        for s in range(SWEEPS + 1)
+    ]
+
+    rim.wait()
     out_node.start()
-    nodes[local - 1].wait()
+    hub.wait()
     inners[0].start()
-    for copy in kinds:
-        copy.wait()
+    kinds.wait()
 
     @pl.when(odd == 1)
     def _():
@@ -90,6 +122,8 @@
     @pl.when(odd == 0)
     def _():
         in_kind.start()
+
+    out_far.start()
 
     def value_at(s, p, c):
         value = at_level(s, p)[c]
@@ -120,13 +154,8 @@
 
     def forward(s, p):
         for c in range(3):
-            value = value_at(s, p, c)
-            moved = shift_next(value, 1)
-            total, jump = value + moved, moved - value
-            moved = shift_next(total, 0)
-            fwd[p + 1, c] = moved - total
-            fwd[p + 1, 6 + c] = moved + total
-            fwd[p + 1, 3 + c] = jump + shift_next(jump, 0)
+            x, y, z = slopes(value_at(s, p, c))
+            fwd[p + 1, c], fwd[p + 1, 3 + c], fwd[p + 1, 6 + c] = x, y, z
 
     def element(e, half=False, into=None):
         lo, hi = e + 1, e + 2
@@ -138,19 +167,9 @@
                 gx = [gx[c] + fwd[lo, c, at, :] for c in range(3)]
                 gy = [gy[c] + fwd[lo, 3 + c, at, :] for c in range(3)]
                 gz = [gz[c] - fwd[lo, 6 + c, at, :] for c in range(3)]
-            bulk = lam[e + 2, at, :] * (gx[0] + gy[1] + gz[2])
-            two, one = mu2[e + 2, at, :], mu[e + 2, at, :]
-            st[to, 0, at, :] = bulk + two * gx[0]
-            st[to, 1, at, :] = bulk + two * gy[1]
-            st[to, 2, at, :] = bulk + two * gz[2]
-            st[to, 3, at, :] = one * (gy[0] + gx[1])
-            st[to, 4, at, :] = one * (gz[0] + gx[2])
-            st[to, 5, at, :] = one * (gz[1] + gy[2])
-
-    def force(px, qy, rz):
-        e = (rz - px) + shift_prev(rz + px, 0)
-        b = qy + shift_prev(qy, 0)
-        return (e - b) + shift_prev(e + b, 1)
+            made = stresses(gx, gy, gz, lam[e + 2, at, :], mu[e + 2, at, :], mu2[e + 2, at, :])
+            for k in range(6):
+                st[to, k, at, :] = made[k]
 
     def internal(p, c):
         lo, hi = p + 1, p + 2
@@ -161,6 +180,9 @@
         return ld[p, c] * sign if c == 2 else ld[p, c]
 
     def settle(s, p, c, value):
+        if p < 0 and s == SWEEPS:
+            rim_u[c] = value
+            return
         u[s - 1, p + 1, c] = value
         if s == SWEEPS and 0 <= p < local:
             out[plane(p), c] = value * sign if c == 2 else value
@@ -190,7 +212,18 @@
         for c in range(3):
             x, y, z = STRESS[c]
             held[s, c] = based(0, c) - force(st[spare, x], st[spare, y], -st[spare, z])
-        pulls[s].start()
+        if s < SWEEPS - 1:
+            pulls[s].start()
+        else:
+            pl.when(closing)(pulls[s].start)
+
+    def leave():
+        element(-1, half=True)
+        for c in range(3):
+            remain = based(0, c) - internal(0, c)
+            rest[plane(0), c] = remain * sign if c == 2 else remain
+        for k, field in enumerate((lam, mu, mu2)):
+            rim_m[k] = field[1]
 
     def outer_part(t):
         if t == -1:
@@ -205,10 +238,12 @@
         if 0 <= t < SWEEPS:
             pulls[t].wait_recv()
             land(t + 1)
-        if -1 <= t < SWEEPS:
+        if -1 <= t < SWEEPS - 1:
             forward(t + 1, -1)
             element(-1)
             advance(t + 2, 0)
+            if t == SWEEPS - 3:
+                pl.when(jnp.logical_not(closing))(pulls[SWEEPS - 1].start)
 
     def middle_part(t):
         if 0 <= t + 2 <= SWEEPS:
@@ -253,41 +288,48 @@
             diagonal(-1)
         if -1 <= t < SWEEPS - 1:
             prepare(t + 2)
-
+        if t == SWEEPS - 2:
+            leave()
+
+    consts.wait()
     for p in range(local - 1):
         material(p)
     for p in range(1, local - 1):
         diagonal(p)
-    for copy in [nodes[p] for p in order[2:]] + bases:
-        copy.wait()
+    middles.wait()
+    bases.wait()
     for t in range(-local - 1, SWEEPS):
         outer_part(t)
         middle_part(t)
         offer_part(t)
-        if t == -3:
-            out_far.start()
         inner_part(t)
         after_part(t)
 
-    out_node.wait_send()
-    out_far.wait_send()
-
-    @pl.when(odd == 1)
-    def _():
-        out_near.wait_send()
-
-    @pl.when(odd == 0)
-    def _():
-        in_kind.wait_send()
-
-    for copy in pulls + inners:
+    for copy in (out_node, out_far, out_near, inners[0]):
         copy.wait_send()
-
-
-def write_out(field, remain, out, rest, sem):
-    copies = [pltpu.make_async_copy(field, out, sem.at[0]), pltpu.make_async_copy(remain, rest, sem.at[1])]
+    remote(held, pull, 0, 0, outer).wait_send()
+    remote(u.at[:, local], u.at[:, local + 1], 1, 0, inner).wait_send()
+
+
+def write_out(field, remain, rim_u, rim_m, out, rest, last, sem):
+    local, _, nx, ny = field.shape
+    odd = lax.rem(lax.axis_index("slab"), 2)
+    sign = (1 - 2 * odd).astype(jnp.float32)
+    copies = [pltpu.make_async_copy(field, out, sem.at[0])]
+    for p in range(1, local):
+        at = plane_of(odd, local, p)
+        copies.append(pltpu.make_async_copy(remain.at[at], rest.at[at], sem.at[p]))
     for copy in copies:
         copy.start()
+    at = plane_of(odd, local, 0)
+    gx, gy, gz = zip(*(slopes(rim_u[c]) for c in range(3)))
+    made = stresses(gx, gy, [-value for value in gz], rim_m[0], rim_m[1], rim_m[2])
+    for c in range(3):
+        x, y, z = STRESS[c]
+        more = force(made[x], made[y], made[z])
+        last[c] = remain[at, c] - (more * sign if c == 2 else more)
+    copies.append(pltpu.make_async_copy(last, rest.at[at], sem.at[local]))
+    copies[-1].start()
     for copy in copies:
         copy.wait()
 
@@ -300,10 +342,11 @@
     vmem = pl.BlockSpec(memory_space=pltpu.VMEM)
     held = pl.pallas_call(
         functools.partial(kernel, peers),
-        out_shape=[pltpu.VMEM(displacement.shape, f32)] * 2,
-        in_specs=[hbm, hbm, hbm, pl.BlockSpec(memory_space=pltpu.SMEM)],
-        out_specs=[vmem, vmem],
+        out_shape=[pltpu.VMEM(displacement.shape, f32)] * 2 + [pltpu.VMEM((comps,) + plane, f32)] * 2,
+        in_specs=[hbm] * 4,
+        out_specs=[vmem] * 4,
         scratch_shapes=[
+            pltpu.SMEM(moduli.shape, f32),
             pltpu.VMEM((local + 2, comps) + plane, f32),
             pltpu.VMEM((SWEEPS, local + 2, comps) + plane, f32),
             pltpu.VMEM((local, comps) + plane, f32),
@@ -317,20 +360,18 @@
             pltpu.VMEM((comps,) + plane, f32),
             pltpu.VMEM((SWEEPS, comps) + plane, f32),
             pltpu.VMEM((SWEEPS, comps) + plane, f32),
-            pltpu.SemaphoreType.DMA((3 * local,)),
-            pltpu.SemaphoreType.DMA((SWEEPS + 3,)),
-            pltpu.SemaphoreType.DMA((SWEEPS + 3,)),
-            pltpu.SemaphoreType.DMA((SWEEPS + 2,)),
-            pltpu.SemaphoreType.DMA((SWEEPS + 2,)),
+            pltpu.SemaphoreType.DMA((6,)),
+            pltpu.SemaphoreType.DMA((6,)),
+            pltpu.SemaphoreType.DMA((SWEEPS + 5,)),
         ],
         compiler_params=pltpu.CompilerParams(collective_id=0, has_side_effects=True),
     )(displacement, load, phase, moduli)
     return pl.pallas_call(
         write_out,
         out_shape=[jax.ShapeDtypeStruct(displacement.shape, f32)] * 2,
-        in_specs=[hbm, hbm],
+        in_specs=[vmem] * 4,
         out_specs=[hbm, hbm],
-        scratch_shapes=[pltpu.SemaphoreType.DMA((2,))],
+        scratch_shapes=[pltpu.VMEM((comps,) + plane, f32), pltpu.SemaphoreType.DMA((local + 1,))],
     )(*[pltpu.with_memory_space_constraint(one, pltpu.VMEM) for one in held])
 
 

time: 25.1 us -> 23.7 us (0.944)
  Pallas kernels: 24.4 us -> 22.9 us
    pallas_call x1, Pallas kernels: 23.5 us -> 22 us  [on_device(): pl.pallas_call(functools.partial(kernel, peers), out_shape=[pltpu.VMEM(di...]
where the time goes in v2:
time: 23.7 us; the launch traced here: 23.6 us
  Pallas kernels  22.9 us (97%)
  between operations  0.64 us (3%)
    pallas_call x1, Pallas kernels, on_device(): pl.pallas_call(functools.partial(kernel, peers), out_shape=[pltpu.VMEM(di...  22 us
    pallas_call x1, Pallas kernels, on_device(): pl.pallas_call(write_out, out_shape=[jax.ShapeDtypeStruct(displacement.sh...  0.94 us

profile of v2, /device:TPU:0, one launch (start us, length us, event | category | flops | bytes accessed | tf_op | source)
XLA Modules:
  0.0 23.6 jit_solution(6157349172827804640)
XLA Ops:
  0.6 22.0 %shard_map.59 = (f32[4,3,32,256]{3,2,1,0:T(8,128)S(1)}, f32[4,3,32,256]{3,2,1,0:T(8,128)S(1)}, f32[3,32,256]{2,1,0:T(8,128)S(1)}, f32[3,32,256]{2,1,0:T(8,128)S(1)}) custom-call(f32[4,3,32,256]{3,2,1,0:T(8,128)} %disp.1, f32[4,3,32,256]{3,2,1,0:T(8,128)} %load.1, s32[4,32,256]{2,1,0:T(8,128)} %phase.1, f32[2,3]{1,0:T(2,128)} %table.1), custom_call_target="tpu_custom_call" | custom-call | tf_op jit(solution)/shard_map/pallas_call | solution.py:343
  22.6 0.9 %shard_map.60 = (f32[4,3,32,256]{3,2,1,0:T(8,128)}, f32[4,3,32,256]{3,2,1,0:T(8,128)}) custom-call(f32[4,3,32,256]{3,2,1,0:T(8,128)S(1)} %get-tuple-element.6.field, f32[4,3,32,256]{3,2,1,0:T(8,128)S(1)} %get-tuple-element.7.remain, f32[3,32,256]{2,1,0:T(8,128)S(1)} %get-tuple-element.8.rim_u, f32[3,32,256]{2,1,0:T(8,128)S(1)} %get-tuple-element.9.rim_m), custom_call_target="tpu_custom_call" | custom-call | tf_op jit(solution)/shard_map/pallas_call | solution.py:369

commit v3 on v2

--- a/solution.py
+++ b/solution.py
@@ -10,6 +10,7 @@
 SWEEPS = 6
 MESH = pl.DeviceIdType.MESH
 ROWS = 8
+LATE = range(SWEEPS // 2, SWEEPS)
 
 STRESS = ((0, 3, 4), (3, 1, 5), (4, 5, 2))
 
@@ -64,6 +65,10 @@
     def plane(p):
         return plane_of(odd, local, p)
 
+    barrier = pltpu.get_barrier_semaphore()
+    for peer in (outer, inner):
+        pl.semaphore_signal(barrier, inc=1, device_id={"slab": peer}, device_id_type=MESH)
+
     def bring(src, dst, at):
         return pltpu.make_async_copy(src, dst, in_sem.at[at])
 
@@ -84,9 +89,6 @@
     for p in range(local):
         bring(load.at[plane(p)], ld.at[p], 5).start()
 
-    barrier = pltpu.get_barrier_semaphore()
-    for peer in (outer, inner):
-        pl.semaphore_signal(barrier, inc=1, device_id={"slab": peer}, device_id_type=MESH)
     pl.semaphore_wait(barrier, 2)
 
     def remote(src, dst, send, recv, peer):
@@ -212,7 +214,7 @@
         for c in range(3):
             x, y, z = STRESS[c]
             held[s, c] = based(0, c) - force(st[spare, x], st[spare, y], -st[spare, z])
-        if s < SWEEPS - 1:
+        if s not in LATE:
             pulls[s].start()
         else:
             pl.when(closing)(pulls[s].start)
@@ -242,8 +244,8 @@
             forward(t + 1, -1)
             element(-1)
             advance(t + 2, 0)
-            if t == SWEEPS - 3:
-                pl.when(jnp.logical_not(closing))(pulls[SWEEPS - 1].start)
+            if t + 2 in LATE[:-1]:
+                pl.when(jnp.logical_not(closing))(pulls[t + 2].start)
 
     def middle_part(t):
         if 0 <= t + 2 <= SWEEPS:
@@ -290,6 +292,8 @@
             prepare(t + 2)
         if t == SWEEPS - 2:
             leave()
+        if t + 2 == LATE[-1]:
+            pl.when(jnp.logical_not(closing))(pulls[t + 2].start)
 
     consts.wait()
     for p in range(local - 1):

time: 23.7 us -> 23.4 us (0.987)
  Pallas kernels: 22.9 us -> 22.6 us
    pallas_call x1, Pallas kernels: 22 us -> 21.7 us  [on_device(): pl.pallas_call(functools.partial(kernel, peers), out_shape=[pltpu.VMEM(di...]
where the time goes in v3:
time: 23.4 us; the launch traced here: 23.3 us
  Pallas kernels  22.6 us (97%)
  between operations  0.64 us (3%)
    pallas_call x1, Pallas kernels, on_device(): pl.pallas_call(functools.partial(kernel, peers), out_shape=[pltpu.VMEM(di...  21.7 us
    pallas_call x1, Pallas kernels, on_device(): pl.pallas_call(write_out, out_shape=[jax.ShapeDtypeStruct(displacement.sh...  0.94 us

profile of v3, /device:TPU:0, one launch (start us, length us, event | category | flops | bytes accessed | tf_op | source)
XLA Modules:
  0.0 23.3 jit_solution(494137851221469451)
XLA Ops:
  0.6 21.7 %shard_map.59 = (f32[4,3,32,256]{3,2,1,0:T(8,128)S(1)}, f32[4,3,32,256]{3,2,1,0:T(8,128)S(1)}, f32[3,32,256]{2,1,0:T(8,128)S(1)}, f32[3,32,256]{2,1,0:T(8,128)S(1)}) custom-call(f32[4,3,32,256]{3,2,1,0:T(8,128)} %disp.1, f32[4,3,32,256]{3,2,1,0:T(8,128)} %load.1, s32[4,32,256]{2,1,0:T(8,128)} %phase.1, f32[2,3]{1,0:T(2,128)} %table.1), custom_call_target="tpu_custom_call" | custom-call | tf_op jit(solution)/shard_map/pallas_call | solution.py:347
  22.3 0.9 %shard_map.60 = (f32[4,3,32,256]{3,2,1,0:T(8,128)}, f32[4,3,32,256]{3,2,1,0:T(8,128)}) custom-call(f32[4,3,32,256]{3,2,1,0:T(8,128)S(1)} %get-tuple-element.6.field, f32[4,3,32,256]{3,2,1,0:T(8,128)S(1)} %get-tuple-element.7.remain, f32[3,32,256]{2,1,0:T(8,128)S(1)} %get-tuple-element.8.rim_u, f32[3,32,256]{2,1,0:T(8,128)S(1)} %get-tuple-element.9.rim_m), custom_call_target="tpu_custom_call" | custom-call | tf_op jit(solution)/shard_map/pallas_call | solution.py:373

commit v4 on v3

--- a/solution.py
+++ b/solution.py
@@ -58,6 +58,7 @@
     me = lax.axis_index("slab")
     odd = lax.rem(me, 2)
     closing = jnp.logical_or(me == 0, me == peers - 1)
+    patient = jnp.logical_and(odd == 0, me > 2)
     sign = (1 - 2 * odd).astype(jnp.float32)
     outer = lax.rem(me + 2 * odd - 1 + peers, peers)
     inner = me + 1 - 2 * odd
@@ -244,8 +245,10 @@
             forward(t + 1, -1)
             element(-1)
             advance(t + 2, 0)
-            if t + 2 in LATE[:-1]:
+            if t + 2 in LATE[:-2]:
                 pl.when(jnp.logical_not(closing))(pulls[t + 2].start)
+            if t + 2 == LATE[-2]:
+                pl.when(jnp.logical_not(jnp.logical_or(closing, patient)))(pulls[t + 2].start)
 
     def middle_part(t):
         if 0 <= t + 2 <= SWEEPS:
@@ -292,6 +295,8 @@
             prepare(t + 2)
         if t == SWEEPS - 2:
             leave()
+        if t + 2 == LATE[-2]:
+            pl.when(patient)(pulls[t + 2].start)
         if t + 2 == LATE[-1]:
             pl.when(jnp.logical_not(closing))(pulls[t + 2].start)
 

time: 23.4 us -> 23.1 us (0.987)
  Pallas kernels: 22.6 us -> 22.1 us
    pallas_call x1, Pallas kernels: 21.7 us -> 21.2 us  [on_device(): pl.pallas_call(functools.partial(kernel, peers), out_shape=[pltpu.VMEM(di...]
where the time goes in v4:
time: 23.1 us; the launch traced here: 22.7 us
  Pallas kernels  22.1 us (96%)
  between operations  0.64 us (3%)
    pallas_call x1, Pallas kernels, on_device(): pl.pallas_call(functools.partial(kernel, peers), out_shape=[pltpu.VMEM(di...  21.2 us
    pallas_call x1, Pallas kernels, on_device(): pl.pallas_call(write_out, out_shape=[jax.ShapeDtypeStruct(displacement.sh...  0.94 us

profile of v4, /device:TPU:0, one launch (start us, length us, event | category | flops | bytes accessed | tf_op | source)
XLA Modules:
  0.0 22.7 jit_solution(606644504997405103)
XLA Ops:
  0.6 21.2 %shard_map.59 = (f32[4,3,32,256]{3,2,1,0:T(8,128)S(1)}, f32[4,3,32,256]{3,2,1,0:T(8,128)S(1)}, f32[3,32,256]{2,1,0:T(8,128)S(1)}, f32[3,32,256]{2,1,0:T(8,128)S(1)}) custom-call(f32[4,3,32,256]{3,2,1,0:T(8,128)} %disp.1, f32[4,3,32,256]{3,2,1,0:T(8,128)} %load.1, s32[4,32,256]{2,1,0:T(8,128)} %phase.1, f32[2,3]{1,0:T(2,128)} %table.1), custom_call_target="tpu_custom_call" | custom-call | tf_op jit(solution)/shard_map/pallas_call | solution.py:352
  21.8 0.9 %shard_map.60 = (f32[4,3,32,256]{3,2,1,0:T(8,128)}, f32[4,3,32,256]{3,2,1,0:T(8,128)}) custom-call(f32[4,3,32,256]{3,2,1,0:T(8,128)S(1)} %get-tuple-element.6.field, f32[4,3,32,256]{3,2,1,0:T(8,128)S(1)} %get-tuple-element.7.remain, f32[3,32,256]{2,1,0:T(8,128)S(1)} %get-tuple-element.8.rim_u, f32[3,32,256]{2,1,0:T(8,128)S(1)} %get-tuple-element.9.rim_m), custom_call_target="tpu_custom_call" | custom-call | tf_op jit(solution)/shard_map/pallas_call | solution.py:378

commit v5 on v4

--- a/solution.py
+++ b/solution.py
@@ -57,7 +57,6 @@
     phases = table.shape[1]
     me = lax.axis_index("slab")
     odd = lax.rem(me, 2)
-    closing = jnp.logical_or(me == 0, me == peers - 1)
     patient = jnp.logical_and(odd == 0, me > 2)
     sign = (1 - 2 * odd).astype(jnp.float32)
     outer = lax.rem(me + 2 * odd - 1 + peers, peers)
@@ -218,7 +217,7 @@
         if s not in LATE:
             pulls[s].start()
         else:
-            pl.when(closing)(pulls[s].start)
+            pl.when(jnp.logical_not(patient))(pulls[s].start)
 
     def leave():
         element(-1, half=True)
@@ -246,9 +245,7 @@
             element(-1)
             advance(t + 2, 0)
             if t + 2 in LATE[:-2]:
-                pl.when(jnp.logical_not(closing))(pulls[t + 2].start)
-            if t + 2 == LATE[-2]:
-                pl.when(jnp.logical_not(jnp.logical_or(closing, patient)))(pulls[t + 2].start)
+                pl.when(patient)(pulls[t + 2].start)
 
     def middle_part(t):
         if 0 <= t + 2 <= SWEEPS:
@@ -295,10 +292,8 @@
             prepare(t + 2)
         if t == SWEEPS - 2:
             leave()
-        if t + 2 == LATE[-2]:
+        if t + 2 in LATE[-2:]:
             pl.when(patient)(pulls[t + 2].start)
-        if t + 2 == LATE[-1]:
-            pl.when(jnp.logical_not(closing))(pulls[t + 2].start)
 
     consts.wait()
     for p in range(local - 1):

time: 23.1 us -> 22.9 us (level)
  no operation moved by 1% of the time
where the time goes in v5:
time: 22.9 us; the launch traced here: 22.7 us
  Pallas kernels  22.1 us (97%)
  between operations  0.64 us (3%)
    pallas_call x1, Pallas kernels, on_device(): pl.pallas_call(functools.partial(kernel, peers), out_shape=[pltpu.VMEM(di...  21.1 us
    pallas_call x1, Pallas kernels, on_device(): pl.pallas_call(write_out, out_shape=[jax.ShapeDtypeStruct(displacement.sh...  0.94 us

profile of v5, /device:TPU:0, one launch (start us, length us, event | category | flops | bytes accessed | tf_op | source)
XLA Modules:
  0.0 22.7 jit_solution(4352776127494893703)
XLA Ops:
  0.6 21.1 %shard_map.59 = (f32[4,3,32,256]{3,2,1,0:T(8,128)S(1)}, f32[4,3,32,256]{3,2,1,0:T(8,128)S(1)}, f32[3,32,256]{2,1,0:T(8,128)S(1)}, f32[3,32,256]{2,1,0:T(8,128)S(1)}) custom-call(f32[4,3,32,256]{3,2,1,0:T(8,128)} %disp.1, f32[4,3,32,256]{3,2,1,0:T(8,128)} %load.1, s32[4,32,256]{2,1,0:T(8,128)} %phase.1, f32[2,3]{1,0:T(2,128)} %table.1), custom_call_target="tpu_custom_call" | custom-call | tf_op jit(solution)/shard_map/pallas_call | solution.py:347
  21.8 0.9 %shard_map.60 = (f32[4,3,32,256]{3,2,1,0:T(8,128)}, f32[4,3,32,256]{3,2,1,0:T(8,128)}) custom-call(f32[4,3,32,256]{3,2,1,0:T(8,128)S(1)} %get-tuple-element.6.field, f32[4,3,32,256]{3,2,1,0:T(8,128)S(1)} %get-tuple-element.7.remain, f32[3,32,256]{2,1,0:T(8,128)S(1)} %get-tuple-element.8.rim_u, f32[3,32,256]{2,1,0:T(8,128)S(1)} %get-tuple-element.9.rim_m), custom_call_target="tpu_custom_call" | custom-call | tf_op jit(solution)/shard_map/pallas_call | solution.py:373

commit v6 on v5

--- a/solution.py
+++ b/solution.py
@@ -76,18 +76,18 @@
         return bring(disp.at[plane(p)], raw.at[p + 1], at)
 
     rim, hub, consts = bring_node(0, 0), bring_node(local - 1, 1), bring(table, moduli, 2)
-    kinds = bring(phase, ph.at[pl.ds(2, local)], 3)
-    middles = bring(disp.at[pl.ds(1, local - 2)], raw.at[pl.ds(2, local - 2)], 4)
-    bases = bring(load, ld, 5)
+    wide = u.at[pl.ds(0, 2), pl.ds(0, local - 1)]
+    rests = bring(wide, wide, 3)
+    early = bring(fwd.at[0, pl.ds(0, 3 + local)], fwd.at[1, pl.ds(0, 3 + local)], 1)
     rim.start()
     hub.start()
     for k in range(local):
-        bring(phase.at[k], ph.at[jnp.where(odd == 1, local - k, k + 2)], 3).start()
+        bring(phase.at[k], ph.at[jnp.where(odd == 1, local - k, k + 2)], 1).start()
     consts.start()
     for p in range(1, local - 1):
-        bring_node(p, 4).start()
+        bring_node(p, 3).start()
     for p in range(local):
-        bring(load.at[plane(p)], ld.at[p], 5).start()
+        bring(load.at[plane(p)], ld.at[p], 3).start()
 
     pl.semaphore_wait(barrier, 2)
 
@@ -97,25 +97,24 @@
             device_id={"slab": peer}, device_id_type=MESH,
         )
 
-    out_node = remote(raw.at[1], raw.at[0], 2, SWEEPS, outer)
-    out_far = remote(ph.at[2], ph.at[0], 3, SWEEPS + 1, outer)
-    out_near = remote(ph.at[1], ph.at[1], 4, SWEEPS + 2, outer)
-    in_kind = remote(ph.at[local + 1], ph.at[local + 1], 4, SWEEPS + 2, inner)
+    out_node = remote(raw.at[1], raw.at[0], 1, SWEEPS, outer)
+    out_far = remote(ph.at[2], ph.at[0], 1, SWEEPS + 1, outer)
+    out_near = remote(ph.at[1], ph.at[1], 1, SWEEPS + 2, outer)
+    in_kind = remote(ph.at[local + 1], ph.at[local + 1], 1, SWEEPS + 2, inner)
     pulls = [remote(held.at[s], pull.at[s], 0, s, outer) for s in range(SWEEPS)]
 
     def at_level(s, p):
         return raw.at[p + 1] if s == 0 else u.at[s - 1, p + 1]
 
     inners = [
-        remote(at_level(s, local - 1), at_level(s, local), 1 if s else 5, SWEEPS + 3 + s % 2, inner)
+        remote(at_level(s, local - 1), at_level(s, local), 0 if s else 1, SWEEPS + 3 + s % 2, inner)
         for s in range(SWEEPS + 1)
     ]
 
     rim.wait()
     out_node.start()
-    hub.wait()
+    early.wait()
     inners[0].start()
-    kinds.wait()
 
     @pl.when(odd == 1)
     def _():
@@ -300,8 +299,7 @@
         material(p)
     for p in range(1, local - 1):
         diagonal(p)
-    middles.wait()
-    bases.wait()
+    rests.wait()
     for t in range(-local - 1, SWEEPS):
         outer_part(t)
         middle_part(t)
@@ -309,10 +307,8 @@
         inner_part(t)
         after_part(t)
 
-    for copy in (out_node, out_far, out_near, inners[0]):
-        copy.wait_send()
-    remote(held, pull, 0, 0, outer).wait_send()
-    remote(u.at[:, local], u.at[:, local + 1], 1, 0, inner).wait_send()
+    remote(fwd.at[0, pl.ds(0, 8)], fwd.at[1, pl.ds(0, 8)], 1, 0, outer).wait_send()
+    remote(u.at[:, pl.ds(0, 2)], u.at[:, pl.ds(0, 2)], 0, 0, outer).wait_send()
 
 
 def write_out(field, remain, rim_u, rim_m, out, rest, last, sem):
@@ -364,8 +360,8 @@
             pltpu.VMEM((comps,) + plane, f32),
             pltpu.VMEM((SWEEPS, comps) + plane, f32),
             pltpu.VMEM((SWEEPS, comps) + plane, f32),
-            pltpu.SemaphoreType.DMA((6,)),
-            pltpu.SemaphoreType.DMA((6,)),
+            pltpu.SemaphoreType.DMA((4,)),
+            pltpu.SemaphoreType.DMA((2,)),
             pltpu.SemaphoreType.DMA((SWEEPS + 5,)),
         ],
         compiler_params=pltpu.CompilerParams(collective_id=0, has_side_effects=True),

time: 22.9 us -> 22.8 us (level)
  no operation moved by 1% of the time
where the time goes in v6:
time: 22.8 us; the launch traced here: 22.7 us
  Pallas kernels  22 us (96%)
  between operations  0.64 us (3%)
    pallas_call x1, Pallas kernels, on_device(): pl.pallas_call(functools.partial(kernel, peers), out_shape=[pltpu.VMEM(di...  21.1 us
    pallas_call x1, Pallas kernels, on_device(): pl.pallas_call(write_out, out_shape=[jax.ShapeDtypeStruct(displacement.sh...  0.94 us

profile of v6, /device:TPU:0, one launch (start us, length us, event | category | flops | bytes accessed | tf_op | source)
XLA Modules:
  0.0 22.7 jit_solution(12514932263311964198)
XLA Ops:
  0.6 21.1 %shard_map.59 = (f32[4,3,32,256]{3,2,1,0:T(8,128)S(1)}, f32[4,3,32,256]{3,2,1,0:T(8,128)S(1)}, f32[3,32,256]{2,1,0:T(8,128)S(1)}, f32[3,32,256]{2,1,0:T(8,128)S(1)}) custom-call(f32[4,3,32,256]{3,2,1,0:T(8,128)} %disp.1, f32[4,3,32,256]{3,2,1,0:T(8,128)} %load.1, s32[4,32,256]{2,1,0:T(8,128)} %phase.1, f32[2,3]{1,0:T(2,128)} %table.1), custom_call_target="tpu_custom_call" | custom-call | tf_op jit(solution)/shard_map/pallas_call | solution.py:343
  21.7 0.9 %shard_map.60 = (f32[4,3,32,256]{3,2,1,0:T(8,128)}, f32[4,3,32,256]{3,2,1,0:T(8,128)}) custom-call(f32[4,3,32,256]{3,2,1,0:T(8,128)S(1)} %get-tuple-element.6.field, f32[4,3,32,256]{3,2,1,0:T(8,128)S(1)} %get-tuple-element.7.remain, f32[3,32,256]{2,1,0:T(8,128)S(1)} %get-tuple-element.8.rim_u, f32[3,32,256]{2,1,0:T(8,128)S(1)} %get-tuple-element.9.rim_m), custom_call_target="tpu_custom_call" | custom-call | tf_op jit(solution)/shard_map/pallas_call | solution.py:369
